TPU v7x, 32 devices: a whole 2x2x4 slice. The times are simulated.
32 devices in a mesh: grp: 4 (over x, core), dev: 8 (over z, y).
Axes of the slice: x: 2, y: 2, z: 4, core: 2. Of those that a mesh axis runs over, the one named last changes fastest.
Arguments:
- node_features: float32 [16384, 768], P(('grp', 'dev')), may hold values from -6 to 6
- tiles: bfloat16 [896, 128, 128], P(('grp', 'dev')), may hold values from -0.1875 to 0.1875
- tile_list: int32 [896, 2], replicated, may hold values from 0 to 127, as said below
- weight: float32 [768, 768], replicated, may hold values from -0.21875 to 0.21875
- texts: float32 [1024, 768], P(('grp', 'dev')), may hold values from -6 to 6
- selected: int32 [1024], P(('grp', 'dev')), may hold values from 0 to 16383, as said below
- pairing: int32 [1024], P(('grp', 'dev')), may hold values from 0 to 1023, each once
Outputs:
- contrast_loss: float32 [], replicated
- grad_nodes: float32 [16384, 768], P(('grp', 'dev'))
- grad_weight: float32 [768, 768], replicated
- grad_texts: float32 [1024, 768], P(('grp', 'dev'))
Inputs may be any that keep to these rules, and one draw needn't show every extreme that they name: `tile_list`: device number p = grp index * (devices along dev) + dev index holds node blocks p * 4 to (p + 1) * 4 - 1 and tiles p * 28 to (p + 1) * 28 - 1. A tile's row block lies on the device that holds the tile; its column block lies on that device, on another device of the same grp index, or on the device of the same dev index in another grp. At most 2 tiles of one device have column blocks on any one other device; in every draw each device has one other device of its grp index and one of its dev index at that most. `selected`: distinct ids; the ids listed on a device are nodes of that device.
All inputs are finite; a program needn't handle non-finite values.
Results may differ from a plain program's by a relative error of at most 0.0004.
The roundings to bfloat16 on the way count: a program that leaves them out, or rounds other values in their place, can miss the bound.
Values may be sent and summed in bfloat16 or wider, within the bound.
No kernel may reach another device: no remote copies, remote signals or barrier semaphores. Data moves between devices by JAX's collectives and lax.ppermute only.
A program may use at most 128 MiB of HBM per device.

v0:
```python
import jax
import jax.numpy as jnp
from jax import lax
from jax.sharding import PartitionSpec as P

CAP = 2
SCALE = 1.0 / 0.07
EPS = 1e-06
PRECISE = lax.Precision.HIGHEST
ROOT_HALF = 0.7071067811865476
INV_ROOT_TWO_PI = 0.3989422804014327


def gelu_value(value):
    return 0.5 * value * (1.0 + lax.erf(value * ROOT_HALF))


def gelu_slope(value):
    return (
        0.5 * (1.0 + lax.erf(value * ROOT_HALF))
        + value * jnp.exp(-0.5 * value * value) * INV_ROOT_TWO_PI
    )


def slot_plan(peer_lists, peer_ids, device, blocks_dev, capacity):
    col_owner = peer_lists[:, :, 1] // blocks_dev
    wanted = (col_owner == device) & (peer_ids[:, None] != device)
    slot_order = jnp.cumsum(wanted.astype(jnp.int32), axis=1) - 1
    local_block = peer_lists[:, :, 1] - device * blocks_dev
    slot_hits = wanted[:, :, None] & (
        slot_order[:, :, None] == jnp.arange(capacity, dtype=jnp.int32)[None, None, :]
    )
    block_index = jnp.sum(jnp.where(slot_hits, local_block[:, :, None], 0), axis=1)
    slot_valid = jnp.any(slot_hits, axis=1)
    return (block_index.reshape(-1), slot_valid.reshape(-1))


def slot_pick(slot_of_tile, keep, slots_all):
    return (slot_of_tile[None, :] == jnp.arange(slots_all, dtype=jnp.int32)[:, None]) & keep[
        None, :
    ]


def land_blocks(total, block_index, valid, incoming):
    return total.at[block_index].add(jnp.where(valid[:, None, None], incoming, 0.0))


def shards(node_features, tiles, tile_list, weight, texts, selected, pairing):
    groups = lax.axis_size("grp")
    members = lax.axis_size("dev")
    grp_index = lax.axis_index("grp")
    dev_index = lax.axis_index("dev")
    device = grp_index * members + dev_index
    block_rows = tiles.shape[1]
    feat_width = node_features.shape[1]
    blocks_dev = node_features.shape[0] // block_rows
    tile_dev = tiles.shape[0]
    sel_dev = selected.shape[0]
    capacity = CAP
    total_sel = sel_dev * groups * members
    rounded = node_features.astype(jnp.bfloat16).reshape(blocks_dev, block_rows, feat_width)
    my_list = lax.dynamic_slice_in_dim(tile_list, device * tile_dev, tile_dev, 0)
    row_block = my_list[:, 0] - device * blocks_dev
    col_owner = my_list[:, 1] // blocks_dev
    col_block = my_list[:, 1] - col_owner * blocks_dev
    owner_grp = col_owner // members
    owner_dev = col_owner % members
    is_local = col_owner == device
    is_near = (owner_grp == grp_index) & jnp.logical_not(is_local)
    is_far = (owner_dev == dev_index) & (owner_grp != grp_index)
    positions = jnp.arange(tile_dev, dtype=jnp.int32)
    earlier = (col_owner[:, None] == col_owner[None, :]) & (positions[None, :] < positions[:, None])
    slot_rank = jnp.sum(earlier.astype(jnp.int32), axis=1)
    near_slot = owner_dev * capacity + slot_rank
    far_slot = owner_grp * capacity + slot_rank
    group_lists = lax.dynamic_slice_in_dim(
        tile_list, grp_index * members * tile_dev, members * tile_dev, 0
    ).reshape(members, tile_dev, 2)
    near_peers = grp_index * members + jnp.arange(members, dtype=jnp.int32)
    near_index, near_valid = slot_plan(group_lists, near_peers, device, blocks_dev, capacity)
    far_lists = lax.dynamic_index_in_dim(
        tile_list.reshape(groups, members, tile_dev, 2), dev_index, 1, False
    )
    far_peers = jnp.arange(groups, dtype=jnp.int32) * members + dev_index
    far_index, far_valid = slot_plan(far_lists, far_peers, device, blocks_dev, capacity)
    zero_half = jnp.zeros((), jnp.bfloat16)
    sel_local = selected - device * blocks_dev * block_rows
    sel_block = sel_local // block_rows
    sel_offset = sel_local % block_rows
    picked = jnp.take(tiles, sel_offset, axis=1)
    tile_rows = jnp.where((row_block[:, None] == sel_block[None, :])[:, :, None], picked, zero_half)
    near_pick = slot_pick(near_slot, is_near, members * capacity)
    far_pick = slot_pick(far_slot, is_far, groups * capacity)
    near_rows = jnp.einsum(
        "st,tkc->skc", near_pick.astype(jnp.bfloat16), tile_rows, preferred_element_type=jnp.float32
    ).astype(jnp.bfloat16)
    far_rows = jnp.einsum(
        "st,tkc->skc", far_pick.astype(jnp.bfloat16), tile_rows, preferred_element_type=jnp.float32
    ).astype(jnp.bfloat16)
    local_tile_rows = jnp.where(is_local[:, None, None], tile_rows, zero_half)
    near_send = jnp.where(
        near_valid[:, None, None], jnp.take(rounded, near_index, axis=0), zero_half
    )
    near_blocks = lax.all_to_all(
        near_send.reshape(members, capacity, block_rows, feat_width),
        "dev",
        split_axis=0,
        concat_axis=0,
        tiled=True,
    )
    far_send = jnp.where(far_valid[:, None, None], jnp.take(rounded, far_index, axis=0), zero_half)
    far_blocks = lax.all_to_all(
        far_send.reshape(groups, capacity, block_rows, feat_width),
        "grp",
        split_axis=0,
        concat_axis=0,
        tiled=True,
    )
    source_table = jnp.concatenate(
        [
            rounded,
            near_blocks.reshape(-1, block_rows, feat_width),
            far_blocks.reshape(-1, block_rows, feat_width),
        ],
        axis=0,
    )
    source_index = jnp.where(
        is_local,
        col_block,
        jnp.where(is_near, blocks_dev + near_slot, blocks_dev + members * capacity + far_slot),
    )
    sources = jnp.take(source_table, source_index, axis=0)
    messages = jnp.einsum("tkc,tcd->kd", tile_rows, sources, preferred_element_type=jnp.float32)
    chosen = node_features[sel_local] + messages
    before = jnp.dot(chosen, weight, precision=PRECISE)
    hidden = gelu_value(before)
    node_norm = jnp.sqrt(jnp.sum(hidden * hidden, axis=1, keepdims=True) + EPS)
    unit_nodes = hidden / node_norm
    text_norm = jnp.sqrt(jnp.sum(texts * texts, axis=1, keepdims=True) + EPS)
    unit_texts = texts / text_norm
    node_rows, pair_rows = (
        lax.all_gather(unit_nodes, "dev", axis=0, tiled=True),
        lax.all_gather(pairing, "dev", axis=0, tiled=True),
    )
    text_cols = lax.all_gather(unit_texts, "grp", axis=0, tiled=True)
    scores = SCALE * lax.dot_general(
        node_rows, text_cols, (((1,), (1,)), ((), ())), precision=PRECISE
    )
    exp_scores = jnp.exp(scores)
    row_total = lax.psum(jnp.sum(exp_scores, axis=1), "dev")
    col_total = lax.psum(jnp.sum(exp_scores, axis=0), "grp")
    col_global = (
        (jnp.arange(groups, dtype=jnp.int32)[:, None] * members + dev_index) * sel_dev
        + jnp.arange(sel_dev, dtype=jnp.int32)[None, :]
    ).reshape(-1)
    target = pair_rows[:, None] == col_global[None, :]
    score_grads = 0.5 * (
        exp_scores / row_total[:, None] + exp_scores / col_total[None, :]
    ) - target.astype(jnp.float32)
    node_part = SCALE * jnp.dot(score_grads, text_cols, precision=PRECISE)
    node_dir = lax.psum_scatter(node_part, "dev", scatter_dimension=0, tiled=True)
    text_part = SCALE * lax.dot_general(
        score_grads, node_rows, (((0,), (0,)), ((), ())), precision=PRECISE
    )
    text_dir = lax.psum_scatter(text_part, "grp", scatter_dimension=0, tiled=True)
    own_rows = lax.dynamic_slice_in_dim(row_total, dev_index * sel_dev, sel_dev, 0)
    own_cols = lax.dynamic_slice_in_dim(col_total, grp_index * sel_dev, sel_dev, 0)
    positive = jnp.sum(jnp.where(target, scores, 0.0))
    lse_sum, pos_sum = lax.psum(
        (jnp.sum(jnp.log(own_rows)) + jnp.sum(jnp.log(own_cols)), positive), ("grp", "dev")
    )
    contrast_loss = lse_sum / (2.0 * total_sel) - pos_sum / total_sel
    node_back = (
        node_dir - unit_nodes * jnp.sum(unit_nodes * node_dir, axis=1, keepdims=True)
    ) / node_norm
    grad_texts = (
        text_dir - unit_texts * jnp.sum(unit_texts * text_dir, axis=1, keepdims=True)
    ) / text_norm
    pre_grad = node_back * gelu_slope(before)
    weight_term = lax.dot_general(chosen, pre_grad, (((0,), (0,)), ((), ())), precision=PRECISE)
    grad_weight = lax.psum(weight_term, ("grp", "dev"))
    row_grads = lax.dot_general(pre_grad, weight, (((1,), (1,)), ((), ())), precision=PRECISE)
    rounded_grads = row_grads.astype(jnp.bfloat16)
    empty_blocks = jnp.zeros((blocks_dev, block_rows, feat_width), jnp.float32)
    local_spread = jnp.einsum(
        "tkc,kd->tcd", local_tile_rows, rounded_grads, preferred_element_type=jnp.float32
    )
    grad_blocks = empty_blocks.at[col_block].add(local_spread)
    near_rows_in = lax.all_to_all(
        near_rows.reshape(members, capacity, sel_dev, block_rows),
        "dev",
        split_axis=0,
        concat_axis=0,
        tiled=True,
    )
    near_grads_in = lax.all_gather(rounded_grads, "dev", axis=0, tiled=True).reshape(
        members, sel_dev, feat_width
    )
    near_spread = jnp.einsum(
        "pqkc,pkd->pqcd", near_rows_in, near_grads_in, preferred_element_type=jnp.float32
    )
    grad_blocks = land_blocks(
        grad_blocks, near_index, near_valid, near_spread.reshape(-1, block_rows, feat_width)
    )
    far_rows_in = lax.all_to_all(
        far_rows.reshape(groups, capacity, sel_dev, block_rows),
        "grp",
        split_axis=0,
        concat_axis=0,
        tiled=True,
    )
    far_grads_in = lax.all_gather(rounded_grads, "grp", axis=0, tiled=True).reshape(
        groups, sel_dev, feat_width
    )
    far_spread = jnp.einsum(
        "pqkc,pkd->pqcd", far_rows_in, far_grads_in, preferred_element_type=jnp.float32
    )
    grad_blocks = land_blocks(
        grad_blocks, far_index, far_valid, far_spread.reshape(-1, block_rows, feat_width)
    )
    grad_nodes = grad_blocks.reshape(-1, feat_width).at[sel_local].add(row_grads)
    return (contrast_loss, grad_nodes, grad_weight, grad_texts)


def solution(mesh):
    return jax.shard_map(
        shards,
        mesh=mesh,
        in_specs=(
            P(("grp", "dev"), None),
            P(("grp", "dev"), None, None),
            P(),
            P(),
            P(("grp", "dev"), None),
            P(("grp", "dev")),
            P(("grp", "dev")),
        ),
        out_specs=(P(), P(("grp", "dev"), None), P(), P(("grp", "dev"), None)),
        check_vma=False,
    )
```

profile of v0, /device:TPU:0, one launch (start us, length us, event | category | flops | bytes accessed | tf_op | source)
XLA Modules:
  0.0 443.1 jit_solution(16403538620831499144)
XLA Ops:
  12.5 2.8 select_select_fusion.1
  15.3 4.4 all-to-all-start.1
  21.1 2.5 gather_fusion.2
  23.9 4.0 select_select_fusion
  27.9 12.5 %all-to-all-done.1 = bf16[4,2,128,768]{3,2,1,0:T(8,128)(2,1)} async-done(((bf16[4,2,128,768]{3,2,1,0:T(8,128)(2,1)}), bf16[4,2,128,768]{3,2,1,0:T(8,128)(2,1)}, u32[]{:S(2)}, u32[]{:S(2)}) %all-to-all-start.1) | async-done | bytes 1572896 | tf_op jit(solution)/shard_map/all_to_all | solution.py:112
  40.4 6.6 %all-to-all-start = ((bf16[8,2,128,768]{3,2,1,0:T(8,128)(2,1)}), bf16[8,2,128,768]{3,2,1,0:T(8,128)(2,1)}, u32[]{:S(2)}, u32[]{:S(2)}) async-start(bf16[8,2,128,768]{3,2,1,0:T(8,128)(2,1)} %select_select_fusion), calls=%async_computation | async-start | bytes 6291456 | tf_op jit(solution)/shard_map/all_to_all | solution.py:104
  50.7 2.8 gather_fusion.1
  53.7 64.1 %all-reduce = s32[256]{0:T(256)S(1)} all-reduce(s32[256]{0:T(256)S(1)} %dynamic-update-slice), channel_id=1, replica_groups=mesh['grp'=4,'dev'=8] {'dev'}, use_global_device_ids=true, to_apply=%add | all-reduce | flops 256 | bytes 2048
  119.0 6.6 %all_gather.16 = f32[128,768]{1,0:T(8,128)} all-gather(f32[32,768]{1,0:T(8,128)S(1)} %broadcast_divide_fusion), channel_id=1, replica_groups=mesh['grp'=4,'dev'=8] {'grp'}, dimensions={0}, use_global_device_ids=true | all-gather | bytes 491520 | tf_op jit(solution)/shard_map/all_gather | solution.py:145
  126.8 5.8 %pad_maximum_fusion = bf16[28,128,768]{2,1,0:T(8,128)(2,1)} fusion(bf16[8,128,768]{2,1,0:T(8,128)(2,1)} %bitcast.17, bf16[16,128,768]{2,1,0:T(8,128)(2,1)} %bitcast.11, bf16[4,128,768]{2,1,0:T(8,128)(2,1)S(1)} %bitcast.101), kind=kLoop, calls=%fused_computation.10 | loop fusion | flops 5505024 | bytes 11010048 | tf_op jit(solution)/shard_map/concatenate | solution.py:119
  132.6 6.0 %gather_fusion.4 = bf16[28,128,768]{2,1,0:T(8,128)(2,1)} fusion(bf16[28,128,768]{2,1,0:T(8,128)(2,1)} %pad_maximum_fusion, s32[1024]{0:T(1024)S(1)} %pad_clamp_fusion), kind=kCustom, calls=%fused_computation.4 | custom fusion | bytes 11010160 | tf_op jit(solution)/shard_map/jit(_take)/gather | solution.py:132
  138.6 3.6 fusion.7
  143.9 32.1 %all_gather.15 = f32[256,768]{1,0:T(8,128)S(1)} all-gather(f32[32,768]{1,0:T(8,128)S(1)} %broadcast_divide_fusion.1), channel_id=1, replica_groups=mesh['grp'=4,'dev'=8] {'dev'}, dimensions={0}, use_global_device_ids=true | all-gather | bytes 884736 | tf_op jit(solution)/shard_map/all_gather | solution.py:142
  178.0 19.6 %psum.35 = f32[256]{0:T(256)S(1)} all-reduce(f32[256]{0:T(256)S(1)} %get-tuple-element.6), channel_id=1, replica_groups=mesh['grp'=4,'dev'=8] {'dev'}, use_global_device_ids=true, to_apply=%region_10.11 | all-reduce | flops 256 | bytes 2048 | tf_op jit(solution)/shard_map/psum | solution.py:150
  197.6 5.6 %psum.36 = f32[128]{0:T(128)S(1)} all-reduce(f32[128]{0:T(128)S(1)} %get-tuple-element.5), channel_id=1, replica_groups=mesh['grp'=4,'dev'=8] {'grp'}, use_global_device_ids=true, to_apply=%region_13.14 | all-reduce | flops 128 | bytes 1024 | tf_op jit(solution)/shard_map/psum | solution.py:151
  203.3 2.3 convolution_multiply_fusion.1
  205.7 2.8 convolution_multiply_fusion
  209.4 3.4 all-to-all-start.2
  216.5 40.7 %all-reduce.1 = (f32[]{:T(128)}, f32[]{:T(128)}) all-reduce(f32[]{:T(128)S(6)} %add.310, f32[]{:T(128)} %get-tuple-element.4), channel_id=1, replica_groups=mesh['grp'=4,'dev'=8] {'grp','dev'}, use_global_device_ids=true, to_apply=%region_15.16 | all-reduce | flops 2 | bytes 16 | tf_op jit(solution)/shard_map/psum | solution.py:169
  261.2 29.5 %reduce-scatter.3.cloned.1.call-done = f32[32,768]{1,0:T(8,128)} async-done(((f32[256,768]{1,0:T(8,128)}), f32[32,768]{1,0:T(8,128)}) %reduce-scatter.3.cloned.1.call-update) | async-done | bytes 98320 | tf_op jit(solution)/shard_map/reduce_scatter | solution.py:161
  291.9 4.4 fusion.57
  298.5 6.1 %fusion.12 = f32[28,128,768]{2,1,0:T(8,128)} fusion(bf16[28,32,128]{2,1,0:T(8,128)(2,1)S(1)} %bitcast_select_fusion.2, pred[28]{0:T(512)(128)(4,1)S(1)} %get-tuple-element.14, bf16[32,768]{1,0:T(8,128)(2,1)S(1)} %get-tuple-element.34), kind=kOutput, calls=%fused_computation.28 | convolution fusion | flops 176275456 | bytes 11288604 | tf_op jit(solution)/shard_map/tkc,kd->tcd/dot_general | solution.py:185
  305.9 25.5 %scatter_fusion = f32[4,128,768]{2,1,0:T(8,128)} fusion(f32[4,128,768]{2,1,0:T(8,128)} %broadcast_in_dim.214, s32[28]{0:T(128)S(1)} %get-tuple-element.15, f32[28,128,768]{2,1,0:T(8,128)} %fusion.12), kind=kCustom, calls=%fused_computation.5 | custom fusion | flops 2752512 | bytes 33030256 | tf_op jit(solution)/shard_map/scatter-add | solution.py:188
  331.4 31.2 %all_gather.18 = bf16[256,768]{1,0:T(8,128)(2,1)S(1)} all-gather(bf16[32,768]{1,0:T(8,128)(2,1)S(1)} %get-tuple-element.34), channel_id=1, replica_groups=mesh['grp'=4,'dev'=8] {'dev'}, dimensions={0}, use_global_device_ids=true | all-gather | bytes 442368 | tf_op jit(solution)/shard_map/all_gather | solution.py:196
  362.5 3.3 all-to-all-start.3
  366.8 3.4 bitcast_select_fusion
  370.2 14.5 %scatter_fusion.1 = f32[4,128,768]{2,1,0:T(8,128)} fusion(f32[4,128,768]{2,1,0:T(8,128)} %scatter_fusion, s32[16]{0:T(128)S(1)} %fusion.47, f32[16,128,768]{2,1,0:T(8,128)} %bitcast_select_fusion), kind=kCustom, calls=%fused_computation.6 | custom fusion | flops 1572864 | bytes 18874432 | tf_op jit(solution)/shard_map/scatter-add | solution.py:45
  384.8 5.8 %all_gather.19 = bf16[128,768]{1,0:T(8,128)(2,1)S(1)} all-gather(bf16[32,768]{1,0:T(8,128)(2,1)S(1)} %get-tuple-element.34), channel_id=1, replica_groups=mesh['grp'=4,'dev'=8] {'grp'}, dimensions={0}, use_global_device_ids=true | all-gather | bytes 245760 | tf_op jit(solution)/shard_map/all_gather | solution.py:212
  393.2 7.4 %scatter_fusion.2 = f32[4,128,768]{2,1,0:T(8,128)} fusion(f32[4,128,768]{2,1,0:T(8,128)} %scatter_fusion.1, s32[8]{0:T(128)S(1)} %fusion.48, f32[8,128,768]{2,1,0:T(8,128)} %bitcast_select_fusion.1), kind=kCustom, calls=%fused_computation.7 | custom fusion | flops 786432 | bytes 9437216 | tf_op jit(solution)/shard_map/scatter-add | solution.py:45
  400.7 3.4 scatter_fusion.3
  404.1 28.1 %all-reduce.4.cloned.1.call-done = f32[768,768]{1,0:T(8,128)} async-done(((f32[768,768]{1,0:T(8,128)}), f32[768,768]{1,0:T(8,128)}) %all-reduce.4.cloned.1.call-update) | async-done | bytes 2359312 | tf_op jit(solution)/shard_map/psum | solution.py:181
  432.2 3.2 copy.43
  (110 shorter events, 30.8 us)
Async XLA Ops:
  7.2 135.0 %copy-start = (f32[768,768]{1,0:T(8,128)S(1)}, f32[768,768]{1,0:T(8,128)}, u32[]{:S(2)}) copy-start(f32[768,768]{1,0:T(8,128)} %param.10) | copy-start | bytes 7077892
  15.3 25.1 %all-to-all-start.1 = ((bf16[4,2,128,768]{3,2,1,0:T(8,128)(2,1)}), bf16[4,2,128,768]{3,2,1,0:T(8,128)(2,1)}, u32[]{:S(2)}, u32[]{:S(2)}) async-start(bf16[4,2,128,768]{3,2,1,0:T(8,128)(2,1)} %select_select_fusion.1), calls=%async_computation.1 | async-start | bytes 3145728 | tf_op jit(solution)/shard_map/all_to_all | solution.py:112
  27.9 19.4 %copy-start.8 = (s32[32]{0:T(128)S(1)}, s32[32]{0:T(128)}, u32[]{:S(2)}) copy-start(s32[32]{0:T(128)} %param.12) | copy-start | bytes 388
  27.9 21.5 %copy-start.10 = (u32[32]{0:T(128)S(1)}, u32[32]{0:T(128)}, u32[]{:S(2)}) copy-start(u32[32]{0:T(128)} %constant.215) | copy-start | bytes 388
  27.9 25.5 %copy-start.9 = (s32[32]{0:T(128)S(1)}, s32[32]{0:T(128)}, u32[]{:S(2)}) copy-start(s32[32]{0:T(128)} %param.13) | copy-start | bytes 388
  27.9 90.8 %copy-start.3 = (f32[32,768]{1,0:T(8,128)S(1)}, f32[32,768]{1,0:T(8,128)}, u32[]{:S(2)}) copy-start(f32[32,768]{1,0:T(8,128)} %param.11) | copy-start | bytes 294916
  40.4 86.4 %all-to-all-start = ((bf16[8,2,128,768]{3,2,1,0:T(8,128)(2,1)}), bf16[8,2,128,768]{3,2,1,0:T(8,128)(2,1)}, u32[]{:S(2)}, u32[]{:S(2)}) async-start(bf16[8,2,128,768]{3,2,1,0:T(8,128)(2,1)} %select_select_fusion), calls=%async_computation | async-start | bytes 6291456 | tf_op jit(solution)/shard_map/all_to_all | solution.py:104
  47.1 211.4 %reduce-scatter.5.cloned.1.call-start = ((), (), s32[]{:S(2)}) async-start(), calls=%async_computation.8 | async-start | bytes 491520 | tf_op jit(solution)/shard_map/reduce_scatter | solution.py:165
  142.2 35.8 %copy-start.6 = (f32[32,768]{1,0:T(8,128)}, f32[32,768]{1,0:T(8,128)S(1)}, u32[]{:S(2)}) copy-start(f32[32,768]{1,0:T(8,128)S(1)} %fusion.7) | copy-start | bytes 294916
  142.2 33.8 %copy-start.2 = (f32[128,768]{1,0:T(8,128)S(1)}, f32[128,768]{1,0:T(8,128)}, u32[]{:S(2)}) copy-start(f32[128,768]{1,0:T(8,128)} %all_gather.16) | copy-start | bytes 1179652
  205.6 52.9 %copy-start.4 = (f32[32,768]{1,0:T(8,128)S(1)}, f32[32,768]{1,0:T(8,128)}, u32[]{:S(2)}) copy-start(f32[32,768]{1,0:T(8,128)} %param.11) | copy-start | bytes 294916
  205.6 86.2 %copy-start.7 = (f32[32,768]{1,0:T(8,128)S(1)}, f32[32,768]{1,0:T(8,128)}, u32[]{:S(2)}) copy-start(f32[32,768]{1,0:T(8,128)} %copy-done.6) | copy-start | bytes 294916
  205.6 85.1 %reduce-scatter.3.cloned.1.call-start = ((), (), s32[]{:S(2)}) async-start(), calls=%async_computation.6 | async-start | bytes 884736 | tf_op jit(solution)/shard_map/reduce_scatter | solution.py:161
  209.4 153.1 %all-to-all-start.2 = ((bf16[8,2,32,128]{3,2,1,0:T(8,128)(2,1)}), bf16[8,2,32,128]{3,2,1,0:T(8,128)(2,1)S(1)}, u32[]{:S(2)}, u32[]{:S(2)}) async-start(bf16[8,2,32,128]{3,2,1,0:T(8,128)(2,1)} %copy.27), calls=%async_computation.3 | async-start | bytes 262144 | tf_op jit(solution)/shard_map/all_to_all | solution.py:189
  212.8 219.4 %all-reduce.4.cloned.1.call-start = ((), (), s32[]{:S(2)}) async-start(), calls=%async_computation.7 | async-start | bytes 4718592 | tf_op jit(solution)/shard_map/psum | solution.py:181
  290.7 5.6 %copy-start.5 = (f32[32,768]{1,0:T(8,128)S(1)}, f32[32,768]{1,0:T(8,128)}, u32[]{:S(2)}) copy-start(f32[32,768]{1,0:T(8,128)} %reduce-scatter.3.cloned.1.call-done) | copy-start | bytes 294916
  362.5 28.0 %all-to-all-start.3 = ((bf16[4,2,32,128]{3,2,1,0:T(8,128)(2,1)}), bf16[4,2,32,128]{3,2,1,0:T(8,128)(2,1)S(1)}, u32[]{:S(2)}, u32[]{:S(2)}) async-start(bf16[4,2,32,128]{3,2,1,0:T(8,128)(2,1)} %copy.30), calls=%async_computation.4 | async-start | bytes 131072 | tf_op jit(solution)/shard_map/all_to_all | solution.py:205
  400.7 34.8 %copy-start.1 = (f32[768,768]{1,0:T(8,128)S(1)}, f32[768,768]{1,0:T(8,128)}, u32[]{:S(2)}) copy-start(f32[768,768]{1,0:T(8,128)} %param.10) | copy-start | bytes 7077892
Sparse Core Ops, SparseCore 0:
  205.7 17.4 reduce-scatter.4
  227.1 63.5 reduce-scatter.2
  296.8 135.3 all-reduce.3
where the time goes:
time: 445 us; the launch traced here: 443 us
  blocking collectives  206 us (46%)
  other arithmetic  78.7 us (18%)
  waiting for transfers between devices  70.1 us (16%)
  matrix products  27 us (6%)
  local copies, waits for them, and re-layouts  25.3 us (6%)
  between operations  18.5 us (4%)
  starting transfers between devices  17.8 us (4%)
    unnamed x1, blocking collectives  64.1 us
    psum x1, blocking collectives, shards(): lax.psum((jnp.sum(jnp.log(own_rows)) + jnp.sum(jnp.log(own_cols)), positi...  40.7 us
    all_gather x1, blocking collectives, shards(): lax.all_gather(unit_nodes, 'dev', axis=0, tiled=True)  32.1 us
    all_gather x1, blocking collectives, shards(): lax.all_gather(rounded_grads, 'dev', axis=0, tiled=True)  31.2 us
    reduce_scatter x1, waiting for transfers between devices, shards(): lax.psum_scatter(node_part, 'dev', scatter_dimension=0, tiled=True)  29.5 us
    psum x1, waiting for transfers between devices, shards(): grad_weight = lax.psum(weight_term, ('grp', 'dev'))  28.1 us
    scatter-add x1, other arithmetic, shards(): grad_blocks = empty_blocks.at[col_block].add(local_spread)  25.5 us
    scatter-add x2, other arithmetic, land_blocks(): total.at[block_index].add(jnp.where(valid[:, None, None], incoming, 0.0))  22 us
  transfers between devices with their start and end apart: 7, of which 3 were waited for; matrix products, arithmetic and copies ran while one was open for 22% of the time, Pallas kernels for 0%

commit v1 on v0

--- a/solution.py
+++ b/solution.py
@@ -178,7 +178,7 @@
     ) / text_norm
     pre_grad = node_back * gelu_slope(before)
     weight_term = lax.dot_general(chosen, pre_grad, (((0,), (0,)), ((), ())), precision=PRECISE)
-    grad_weight = lax.psum(weight_term, ("grp", "dev"))
+    grad_weight = lax.psum(lax.psum(weight_term, "dev"), "grp")
     row_grads = lax.dot_general(pre_grad, weight, (((1,), (1,)), ((), ())), precision=PRECISE)
     rounded_grads = row_grads.astype(jnp.bfloat16)
     empty_blocks = jnp.zeros((blocks_dev, block_rows, feat_width), jnp.float32)

time: 445 us -> 475 us (1.067)
  waiting for transfers between devices: 70.1 us -> 88.6 us
    reduce_scatter x1, waiting for transfers between devices: 29.5 us -> 57.5 us  [shards(): lax.psum_scatter(node_part, 'dev', scatter_dimension=0, tiled=True)]
    psum x1 -> x2, waiting for transfers between devices: 28.1 us -> 18.5 us  [shards(): grad_weight = lax.psum(lax.psum(weight_term, 'dev'), 'grp')]
  transfers between devices with their start and end apart: 7 -> 8, of which waited for: 3 -> 4; matrix products, arithmetic and copies ran while one was open for 22% -> 22% of each run, Pallas kernels for 0% -> 0%
where the time goes in v1:
time: 475 us; the launch traced here: 473 us
  blocking collectives  210 us (44%)
  waiting for transfers between devices  88.6 us (19%)
  other arithmetic  81.8 us (17%)
  matrix products  29.8 us (6%)
  local copies, waits for them, and re-layouts  25.3 us (5%)
  starting transfers between devices  18.7 us (4%)
  between operations  18.5 us (4%)
    unnamed x1, blocking collectives  64.1 us
    reduce_scatter x1, waiting for transfers between devices, shards(): lax.psum_scatter(node_part, 'dev', scatter_dimension=0, tiled=True)  57.5 us
    psum x1, blocking collectives, shards(): lax.psum((jnp.sum(jnp.log(own_rows)) + jnp.sum(jnp.log(own_cols)), positi...  43 us
    all_gather x1, blocking collectives, shards(): lax.all_gather(rounded_grads, 'dev', axis=0, tiled=True)  32.4 us
    all_gather x1, blocking collectives, shards(): lax.all_gather(unit_nodes, 'dev', axis=0, tiled=True)  32.1 us
    scatter-add x1, other arithmetic, shards(): grad_blocks = empty_blocks.at[col_block].add(local_spread)  25.4 us
    scatter-add x2, other arithmetic, land_blocks(): total.at[block_index].add(jnp.where(valid[:, None, None], incoming, 0.0))  22.4 us
    psum x1, blocking collectives, shards(): row_total = lax.psum(jnp.sum(exp_scores, axis=1), 'dev')  19.6 us
  transfers between devices with their start and end apart: 8, of which 4 were waited for; matrix products, arithmetic and copies ran while one was open for 22% of the time, Pallas kernels for 0%

profile of v1, /device:TPU:0, one launch (start us, length us, event | category | flops | bytes accessed | tf_op | source)
XLA Modules:
  0.0 473.2 jit_solution(13719974545332323516)
XLA Ops:
  12.5 2.8 select_select_fusion.1
  15.3 4.4 all-to-all-start.1
  21.1 2.5 gather_fusion.2
  23.9 4.0 select_select_fusion
  27.9 12.5 %all-to-all-done.1 = bf16[4,2,128,768]{3,2,1,0:T(8,128)(2,1)} async-done(((bf16[4,2,128,768]{3,2,1,0:T(8,128)(2,1)}), bf16[4,2,128,768]{3,2,1,0:T(8,128)(2,1)}, u32[]{:S(2)}, u32[]{:S(2)}) %all-to-all-start.1) | async-done | bytes 1572896 | tf_op jit(solution)/shard_map/all_to_all | solution.py:112
  40.4 6.6 %all-to-all-start = ((bf16[8,2,128,768]{3,2,1,0:T(8,128)(2,1)}), bf16[8,2,128,768]{3,2,1,0:T(8,128)(2,1)}, u32[]{:S(2)}, u32[]{:S(2)}) async-start(bf16[8,2,128,768]{3,2,1,0:T(8,128)(2,1)} %select_select_fusion), calls=%async_computation | async-start | bytes 6291456 | tf_op jit(solution)/shard_map/all_to_all | solution.py:104
  50.7 2.8 gather_fusion.1
  53.7 64.1 %all-reduce = s32[256]{0:T(256)S(1)} all-reduce(s32[256]{0:T(256)S(1)} %dynamic-update-slice), channel_id=1, replica_groups=mesh['grp'=4,'dev'=8] {'dev'}, use_global_device_ids=true, to_apply=%add | all-reduce | flops 256 | bytes 2048
  119.0 6.6 %all_gather.16 = f32[128,768]{1,0:T(8,128)} all-gather(f32[32,768]{1,0:T(8,128)S(1)} %broadcast_divide_fusion), channel_id=1, replica_groups=mesh['grp'=4,'dev'=8] {'grp'}, dimensions={0}, use_global_device_ids=true | all-gather | bytes 491520 | tf_op jit(solution)/shard_map/all_gather | solution.py:145
  126.8 5.8 %pad_maximum_fusion = bf16[28,128,768]{2,1,0:T(8,128)(2,1)} fusion(bf16[8,128,768]{2,1,0:T(8,128)(2,1)} %bitcast.17, bf16[16,128,768]{2,1,0:T(8,128)(2,1)} %bitcast.11, bf16[4,128,768]{2,1,0:T(8,128)(2,1)S(1)} %bitcast.101), kind=kLoop, calls=%fused_computation.10 | loop fusion | flops 5505024 | bytes 11010048 | tf_op jit(solution)/shard_map/concatenate | solution.py:119
  132.6 6.0 %gather_fusion.4 = bf16[28,128,768]{2,1,0:T(8,128)(2,1)} fusion(bf16[28,128,768]{2,1,0:T(8,128)(2,1)} %pad_maximum_fusion, s32[1024]{0:T(1024)S(1)} %pad_clamp_fusion), kind=kCustom, calls=%fused_computation.4 | custom fusion | bytes 11010160 | tf_op jit(solution)/shard_map/jit(_take)/gather | solution.py:132
  138.6 3.6 fusion.7
  143.9 32.1 %all_gather.15 = f32[256,768]{1,0:T(8,128)S(1)} all-gather(f32[32,768]{1,0:T(8,128)S(1)} %broadcast_divide_fusion.1), channel_id=1, replica_groups=mesh['grp'=4,'dev'=8] {'dev'}, dimensions={0}, use_global_device_ids=true | all-gather | bytes 884736 | tf_op jit(solution)/shard_map/all_gather | solution.py:142
  178.0 19.6 %psum.42 = f32[256]{0:T(256)S(1)} all-reduce(f32[256]{0:T(256)S(1)} %get-tuple-element.6), channel_id=1, replica_groups=mesh['grp'=4,'dev'=8] {'dev'}, use_global_device_ids=true, to_apply=%region_10.11 | all-reduce | flops 256 | bytes 2048 | tf_op jit(solution)/shard_map/psum | solution.py:150
  197.7 5.6 %psum.43 = f32[128]{0:T(128)S(1)} all-reduce(f32[128]{0:T(128)S(1)} %get-tuple-element.5), channel_id=1, replica_groups=mesh['grp'=4,'dev'=8] {'grp'}, use_global_device_ids=true, to_apply=%region_13.14 | all-reduce | flops 128 | bytes 1024 | tf_op jit(solution)/shard_map/psum | solution.py:151
  203.3 2.8 convolution_multiply_fusion
  208.6 57.5 %reduce-scatter.3.cloned.1.call-done = f32[32,768]{1,0:T(8,128)} async-done(((f32[256,768]{1,0:T(8,128)}), f32[32,768]{1,0:T(8,128)}) %reduce-scatter.3.cloned.1.call-update) | async-done | bytes 98320 | tf_op jit(solution)/shard_map/reduce_scatter | solution.py:161
  267.2 4.5 fusion.57
  272.6 3.7 all-to-all-start.2
  279.9 43.0 %all-reduce.1 = (f32[]{:T(128)}, f32[]{:T(128)}) all-reduce(f32[]{:T(128)S(6)} %add.312, f32[]{:T(128)} %get-tuple-element.4), channel_id=1, replica_groups=mesh['grp'=4,'dev'=8] {'grp','dev'}, use_global_device_ids=true, to_apply=%region_15.16 | all-reduce | flops 2 | bytes 16 | tf_op jit(solution)/shard_map/psum | solution.py:169
  329.3 6.1 %fusion.12 = f32[28,128,768]{2,1,0:T(8,128)} fusion(bf16[28,32,128]{2,1,0:T(8,128)(2,1)S(1)} %bitcast_select_fusion.2, pred[28]{0:T(512)(128)(4,1)S(1)} %get-tuple-element.14, bf16[32,768]{1,0:T(8,128)(2,1)S(1)} %get-tuple-element.34), kind=kOutput, calls=%fused_computation.28 | convolution fusion | flops 176275456 | bytes 11288604 | tf_op jit(solution)/shard_map/tkc,kd->tcd/dot_general | solution.py:185
  336.6 25.4 %scatter_fusion = f32[4,128,768]{2,1,0:T(8,128)} fusion(f32[4,128,768]{2,1,0:T(8,128)} %broadcast_in_dim.214, s32[28]{0:T(128)S(1)} %get-tuple-element.15, f32[28,128,768]{2,1,0:T(8,128)} %fusion.12), kind=kCustom, calls=%fused_computation.5 | custom fusion | flops 2752512 | bytes 33030256 | tf_op jit(solution)/shard_map/scatter-add | solution.py:188
  362.0 32.4 %all_gather.18 = bf16[256,768]{1,0:T(8,128)(2,1)S(1)} all-gather(bf16[32,768]{1,0:T(8,128)(2,1)S(1)} %get-tuple-element.34), channel_id=1, replica_groups=mesh['grp'=4,'dev'=8] {'dev'}, dimensions={0}, use_global_device_ids=true | all-gather | bytes 442368 | tf_op jit(solution)/shard_map/all_gather | solution.py:196
  394.5 3.8 all-to-all-start.3
  398.3 3.7 fusion.64
  403.5 6.1 %bitcast_select_fusion = f32[16,128,768]{2,1,0:T(8,128)} fusion(f32[8,2,128,768]{3,2,1,0:T(8,128)} %fusion.64, pred[16]{0:T(512)(128)(4,1)S(1)} %broadcast_in_dim.216), kind=kLoop, calls=%fused_computation.9 | loop fusion | flops 1572864 | bytes 12582928 | tf_op jit(solution)/shard_map/jit(_where)/select_n | solution.py:45
  409.6 14.9 %scatter_fusion.1 = f32[4,128,768]{2,1,0:T(8,128)} fusion(f32[4,128,768]{2,1,0:T(8,128)} %scatter_fusion, s32[16]{0:T(128)S(1)} %fusion.47, f32[16,128,768]{2,1,0:T(8,128)} %bitcast_select_fusion), kind=kCustom, calls=%fused_computation.6 | custom fusion | flops 1572864 | bytes 18874432 | tf_op jit(solution)/shard_map/scatter-add | solution.py:45
  424.5 7.1 %all_gather.19 = bf16[128,768]{1,0:T(8,128)(2,1)S(1)} all-gather(bf16[32,768]{1,0:T(8,128)(2,1)S(1)} %get-tuple-element.34), channel_id=1, replica_groups=mesh['grp'=4,'dev'=8] {'grp'}, dimensions={0}, use_global_device_ids=true | all-gather | bytes 245760 | tf_op jit(solution)/shard_map/all_gather | solution.py:212
  434.2 7.5 %scatter_fusion.2 = f32[4,128,768]{2,1,0:T(8,128)} fusion(f32[4,128,768]{2,1,0:T(8,128)} %scatter_fusion.1, s32[8]{0:T(128)S(1)} %fusion.48, f32[8,128,768]{2,1,0:T(8,128)} %bitcast_select_fusion.1), kind=kCustom, calls=%fused_computation.7 | custom fusion | flops 786432 | bytes 9437216 | tf_op jit(solution)/shard_map/scatter-add | solution.py:45
  441.7 3.5 scatter_fusion.3
  445.3 17.0 %all-reduce.7.cloned.1.call-done = f32[768,768]{1,0:T(8,128)} async-done(((f32[768,768]{1,0:T(8,128)}), f32[768,768]{1,0:T(8,128)}) %all-reduce.7.cloned.1.call-update) | async-done | bytes 2359312 | tf_op jit(solution)/shard_map/psum | solution.py:181
  462.3 3.2 copy.44
  (111 shorter events, 33.5 us)
Async XLA Ops:
  7.2 135.0 %copy-start = (f32[768,768]{1,0:T(8,128)S(1)}, f32[768,768]{1,0:T(8,128)}, u32[]{:S(2)}) copy-start(f32[768,768]{1,0:T(8,128)} %param.10) | copy-start | bytes 7077892
  15.3 25.1 %all-to-all-start.1 = ((bf16[4,2,128,768]{3,2,1,0:T(8,128)(2,1)}), bf16[4,2,128,768]{3,2,1,0:T(8,128)(2,1)}, u32[]{:S(2)}, u32[]{:S(2)}) async-start(bf16[4,2,128,768]{3,2,1,0:T(8,128)(2,1)} %select_select_fusion.1), calls=%async_computation.1 | async-start | bytes 3145728 | tf_op jit(solution)/shard_map/all_to_all | solution.py:112
  27.9 19.4 %copy-start.7 = (s32[32]{0:T(128)S(1)}, s32[32]{0:T(128)}, u32[]{:S(2)}) copy-start(s32[32]{0:T(128)} %param.12) | copy-start | bytes 388
  27.9 21.5 %copy-start.9 = (u32[32]{0:T(128)S(1)}, u32[32]{0:T(128)}, u32[]{:S(2)}) copy-start(u32[32]{0:T(128)} %constant.215) | copy-start | bytes 388
  27.9 25.5 %copy-start.8 = (s32[32]{0:T(128)S(1)}, s32[32]{0:T(128)}, u32[]{:S(2)}) copy-start(s32[32]{0:T(128)} %param.13) | copy-start | bytes 388
  27.9 90.8 %copy-start.3 = (f32[32,768]{1,0:T(8,128)S(1)}, f32[32,768]{1,0:T(8,128)}, u32[]{:S(2)}) copy-start(f32[32,768]{1,0:T(8,128)} %param.11) | copy-start | bytes 294916
  40.4 86.4 %all-to-all-start = ((bf16[8,2,128,768]{3,2,1,0:T(8,128)(2,1)}), bf16[8,2,128,768]{3,2,1,0:T(8,128)(2,1)}, u32[]{:S(2)}, u32[]{:S(2)}) async-start(bf16[8,2,128,768]{3,2,1,0:T(8,128)(2,1)} %select_select_fusion), calls=%async_computation | async-start | bytes 6291456 | tf_op jit(solution)/shard_map/all_to_all | solution.py:104
  47.1 219.0 %reduce-scatter.3.cloned.1.call-start = ((), (), s32[]{:S(2)}) async-start(), calls=%async_computation.6 | async-start | bytes 884736 | tf_op jit(solution)/shard_map/reduce_scatter | solution.py:161
  142.2 35.8 %copy-start.6 = (f32[32,768]{1,0:T(8,128)}, f32[32,768]{1,0:T(8,128)S(1)}, u32[]{:S(2)}) copy-start(f32[32,768]{1,0:T(8,128)S(1)} %fusion.7) | copy-start | bytes 294916
  142.2 33.8 %copy-start.2 = (f32[128,768]{1,0:T(8,128)S(1)}, f32[128,768]{1,0:T(8,128)}, u32[]{:S(2)}) copy-start(f32[128,768]{1,0:T(8,128)} %all_gather.16) | copy-start | bytes 1179652
  206.1 118.1 %reduce-scatter.5.cloned.1.call-start = ((), (), s32[]{:S(2)}) async-start(), calls=%async_computation.9 | async-start | bytes 491520 | tf_op jit(solution)/shard_map/reduce_scatter | solution.py:165
  208.5 194.9 %all-reduce.5.cloned.1.call-start = ((), (), s32[]{:S(2)}) async-start(), calls=%async_computation.7 | async-start | bytes 4718592 | tf_op jit(solution)/shard_map/psum | solution.py:181
  267.2 57.1 %copy-start.4 = (f32[32,768]{1,0:T(8,128)S(1)}, f32[32,768]{1,0:T(8,128)}, u32[]{:S(2)}) copy-start(f32[32,768]{1,0:T(8,128)} %param.11) | copy-start | bytes 294916
  267.2 59.8 %copy-start.5 = (f32[32,768]{1,0:T(8,128)S(1)}, f32[32,768]{1,0:T(8,128)}, u32[]{:S(2)}) copy-start(f32[32,768]{1,0:T(8,128)} %reduce-scatter.3.cloned.1.call-done) | copy-start | bytes 294916
  272.6 121.9 %all-to-all-start.2 = ((bf16[8,2,32,128]{3,2,1,0:T(8,128)(2,1)}), bf16[8,2,32,128]{3,2,1,0:T(8,128)(2,1)S(1)}, u32[]{:S(2)}, u32[]{:S(2)}) async-start(bf16[8,2,32,128]{3,2,1,0:T(8,128)(2,1)} %copy.27), calls=%async_computation.3 | async-start | bytes 262144 | tf_op jit(solution)/shard_map/all_to_all | solution.py:189
  394.5 37.1 %all-to-all-start.3 = ((bf16[4,2,32,128]{3,2,1,0:T(8,128)(2,1)}), bf16[4,2,32,128]{3,2,1,0:T(8,128)(2,1)S(1)}, u32[]{:S(2)}, u32[]{:S(2)}) async-start(bf16[4,2,32,128]{3,2,1,0:T(8,128)(2,1)} %copy.30), calls=%async_computation.4 | async-start | bytes 131072 | tf_op jit(solution)/shard_map/all_to_all | solution.py:205
  398.3 64.0 %all-reduce.7.cloned.1.call-start = ((), (), s32[]{:S(2)}) async-start(), calls=%async_computation.8 | async-start | bytes 4718592 | tf_op jit(solution)/shard_map/psum | solution.py:181
  441.7 23.8 %copy-start.1 = (f32[768,768]{1,0:T(8,128)S(1)}, f32[768,768]{1,0:T(8,128)}, u32[]{:S(2)}) copy-start(f32[768,768]{1,0:T(8,128)} %param.10) | copy-start | bytes 7077892
Sparse Core Ops, SparseCore 0:
  206.2 59.8 reduce-scatter.2
  268.6 20.0 reduce-scatter.4
  292.9 110.5 all-reduce.4
  405.7 56.5 all-reduce.6
